TPU v7x, 32 devices: a whole 2x2x4 slice. The times are simulated.
32 devices in a mesh: cz: 4 (over z), cy: 2 (over y), cx: 4 (over x, core).
Axes of the slice: x: 2, y: 2, z: 4, core: 2. Of those that a mesh axis runs over, the one named last changes fastest.
Arguments:
- x: bfloat16 [1024, 5120], P(('cx', 'cz'), 'cy')
- w1: bfloat16 [5120, 20480], P('cy', ('cz', 'cx'))
- w2: bfloat16 [20480, 5120], P('cz', ('cy', 'cx'))
Outputs:
- output: bfloat16 [1024, 5120], P(('cx', 'cz'), 'cy')
All inputs are finite; a program needn't handle non-finite values.
Results may differ from a plain program's by a relative error of at most 0.0115024.
Values are sent between devices in bfloat16 or wider.
A program may use at most 1 GiB of HBM per device.

v0:
```python
import jax
import jax.numpy as jnp
from jax import lax
from jax.sharding import PartitionSpec as P


def solution(mesh):
    def body(x, w1, w2):
        xg = lax.all_gather(x, "cz", axis=0, tiled=True)
        w1g = lax.all_gather(w1, "cx", axis=1, tiled=True)
        cp = jnp.dot(xg, w1g, preferred_element_type=jnp.float32)
        c = lax.psum_scatter(cp, "cy", scatter_dimension=0, tiled=True).astype(jnp.bfloat16)
        h = jax.nn.gelu(c.astype(jnp.float32), approximate=True).astype(jnp.bfloat16)
        hg = lax.all_gather(h, "cy", axis=0, tiled=True)
        w2g = lax.all_gather(w2, "cx", axis=1, tiled=True)
        zp = jnp.dot(hg, w2g, preferred_element_type=jnp.float32)
        return lax.psum_scatter(zp, "cz", scatter_dimension=0, tiled=True).astype(jnp.bfloat16)

    return jax.shard_map(
        body,
        mesh=mesh,
        in_specs=(P(("cx", "cz"), "cy"), P("cy", ("cz", "cx")), P("cz", ("cy", "cx"))),
        out_specs=P(("cx", "cz"), "cy"),
        check_vma=False,
    )
```

profile of v0, /device:TPU:0, one launch (start us, length us, event | category | flops | bytes accessed | tf_op | source)
XLA Modules:
  0.0 563.8 jit_solution(64054820711711165)
XLA Ops:
  6.5 0.0 all-gather.5.cloned.1.call-start
  6.5 0.7 all-gather.5.cloned.1.call-update
  7.3 0.0 all-gather.7.cloned.1.call-start
  7.3 0.7 all-gather.7.cloned.1.call-update
  8.0 0.0 reduce-scatter.3.cloned.1.call-start
  8.1 35.8 %all-gather.5.cloned.1.call-done = bf16[256,2560]{1,0:T(8,128)(2,1)} async-done(((bf16[64,2560]{1,0:T(8,128)(2,1)}), bf16[256,2560]{1,0:T(8,128)(2,1)}) %all-gather.5.cloned.1.call-update) | async-done | bytes 1310736 | tf_op jit(solution)/shard_map/all_gather | solution.py:9
  43.9 162.3 %all-gather.7.cloned.1.call-done = bf16[2560,5120]{1,0:T(8,128)(2,1)} async-done(((bf16[2560,1280]{1,0:T(8,128)(2,1)}), bf16[2560,5120]{1,0:T(8,128)(2,1)}) %all-gather.7.cloned.1.call-update) | async-done | bytes 26214416 | tf_op jit(solution)/shard_map/all_gather | solution.py:10
  206.2 13.9 %fusion.6 = f32[256,5120]{1,0:T(8,128)} fusion(bf16[256,2560]{1,0:T(8,128)(2,1)} %all-gather.5.cloned.1.call-done, bf16[2560,5120]{1,0:T(8,128)(2,1)} %all-gather.7.cloned.1.call-done), kind=kOutput, calls=%fused_computation.10 | convolution fusion | flops 6710886400 | bytes 32768000 | tf_op jit(solution)/shard_map/dot_general | solution.py:11
  220.0 0.0 reduce-scatter.3.cloned.1.call-update
  220.0 0.0 all-gather.11.cloned.1.call-start
  220.1 0.5 all-gather.11.cloned.1.call-update
  220.6 0.0 all-gather.9.cloned.1.call-start
  220.7 65.2 %reduce-scatter.3.cloned.1.call-done = f32[128,5120]{1,0:T(8,128)} async-done(((f32[256,5120]{1,0:T(8,128)}), f32[128,5120]{1,0:T(8,128)}) %reduce-scatter.3.cloned.1.call-update) | async-done | bytes 2621456 | tf_op jit(solution)/shard_map/reduce_scatter | solution.py:12
  285.8 3.7 fusion.5
  289.5 0.0 all-gather.9.cloned.1.call-update
  289.5 0.0 reduce-scatter.5.cloned.1.call-start
  289.6 158.9 %all-gather.11.cloned.1.call-done = bf16[5120,2560]{1,0:T(8,128)(2,1)} async-done(((bf16[5120,640]{1,0:T(8,128)(2,1)}), bf16[5120,2560]{1,0:T(8,128)(2,1)}) %all-gather.11.cloned.1.call-update) | async-done | bytes 26214416 | tf_op jit(solution)/shard_map/all_gather | solution.py:15
  448.5 40.4 %all-gather.9.cloned.1.call-done = bf16[256,5120]{1,0:T(8,128)(2,1)} async-done(((bf16[128,5120]{1,0:T(8,128)(2,1)}), bf16[256,5120]{1,0:T(8,128)(2,1)}) %all-gather.9.cloned.1.call-update) | async-done | bytes 2621456 | tf_op jit(solution)/shard_map/all_gather | solution.py:14
  488.9 13.8 %fusion.7 = f32[256,2560]{1,0:T(8,128)} fusion(bf16[256,5120]{1,0:T(8,128)(2,1)} %all-gather.9.cloned.1.call-done, bf16[5120,2560]{1,0:T(8,128)(2,1)} %all-gather.11.cloned.1.call-done), kind=kOutput, calls=%fused_computation.11 | convolution fusion | flops 6710886400 | bytes 31457280 | tf_op jit(solution)/shard_map/dot_general | solution.py:16
  502.7 0.0 reduce-scatter.5.cloned.1.call-update
  502.7 52.4 %reduce-scatter.5.cloned.1.call-done = f32[64,2560]{1,0:T(8,128)} async-done(((f32[256,2560]{1,0:T(8,128)}), f32[64,2560]{1,0:T(8,128)}) %reduce-scatter.5.cloned.1.call-update) | async-done | bytes 655376 | tf_op jit(solution)/shard_map/reduce_scatter | solution.py:17
  555.2 1.8 convert_element_type.15
Async XLA Ops:
  6.5 37.3 %all-gather.5.cloned.1.call-start = ((), (), s32[]{:S(2)}) async-start(), calls=%async_computation.2 | async-start | bytes 1638400 | tf_op jit(solution)/shard_map/all_gather | solution.py:9
  7.3 198.9 %all-gather.7.cloned.1.call-start = ((), (), s32[]{:S(2)}) async-start(), calls=%async_computation.3 | async-start | bytes 32768000 | tf_op jit(solution)/shard_map/all_gather | solution.py:10
  8.0 277.8 %reduce-scatter.3.cloned.1.call-start = ((), (), s32[]{:S(2)}) async-start(), calls=%async_computation.4 | async-start | bytes 7864320 | tf_op jit(solution)/shard_map/reduce_scatter | solution.py:12
  220.0 228.5 %all-gather.11.cloned.1.call-start = ((), (), s32[]{:S(2)}) async-start(), calls=%async_computation.6 | async-start | bytes 32768000 | tf_op jit(solution)/shard_map/all_gather | solution.py:15
  220.6 268.2 %all-gather.9.cloned.1.call-start = ((), (), s32[]{:S(2)}) async-start(), calls=%async_computation.5 | async-start | bytes 3932160 | tf_op jit(solution)/shard_map/all_gather | solution.py:14
  289.5 265.6 %reduce-scatter.5.cloned.1.call-start = ((), (), s32[]{:S(2)}) async-start(), calls=%async_computation.7 | async-start | bytes 3276800 | tf_op jit(solution)/shard_map/reduce_scatter | solution.py:17
Sparse Core Ops, SparseCore 0:
  8.9 34.9 all-gather.4
  45.4 160.6 all-gather.6
  220.2 65.6 reduce-scatter.2
  287.3 161.1 all-gather.10
  449.9 38.9 all-gather.8
  502.8 52.2 reduce-scatter.4
where the time goes:
time: 564 us
  waiting for transfers between devices  517 us (92%)
  matrix products  27.7 us (5%)
  between operations  13.5 us (2%)
    all_gather x1, waiting for transfers between devices, body(): w1g = lax.all_gather(w1, 'cx', axis=1, tiled=True)  162 us
    all_gather x1, waiting for transfers between devices, body(): w2g = lax.all_gather(w2, 'cx', axis=1, tiled=True)  159 us
    reduce_scatter x1, waiting for transfers between devices, body(): lax.psum_scatter(cp, 'cy', scatter_dimension=0, tiled=True)  65.2 us
    reduce_scatter x1, waiting for transfers between devices, body(): lax.psum_scatter(zp, 'cz', scatter_dimension=0, tiled=True)  52.4 us
    all_gather x1, waiting for transfers between devices, body(): hg = lax.all_gather(h, 'cy', axis=0, tiled=True)  40.4 us
    all_gather x1, waiting for transfers between devices, body(): xg = lax.all_gather(x, 'cz', axis=0, tiled=True)  35.8 us
    dot_general x1, matrix products, body(): cp = jnp.dot(xg, w1g, preferred_element_type=jnp.float32)  13.9 us
    dot_general x1, matrix products, body(): zp = jnp.dot(hg, w2g, preferred_element_type=jnp.float32)  13.8 us
  transfers between devices with their start and end apart: 6, of which 6 were waited for; matrix products, arithmetic and copies ran while one was open for 1% of the time, Pallas kernels for 0%

commit v1 on v0

v1 whole, which is shorter than its diff:
```python
import functools

import jax
import jax.numpy as jnp
from jax import lax
from jax.experimental import pallas as pl
from jax.experimental.pallas import tpu as pltpu
from jax.sharding import PartitionSpec as P

MESH = pl.DeviceIdType.MESH
LH, LF, LC, L2 = 1, 2, 3, 4
STEPS = 16 + L2 + 1


def kernel(x_ref, w1_ref, w2_ref, o_ref, w1s, w1o, w2, xb, cs, co, cr, hb, zp, zu, zd, ob,
           wsem, xxs, xxr, xus, xds, xzr, xc0s, xc1s, xc2s, xcr, css, crr, hys, hyr, hx0s, hx0r, hx1s, hx1r,
           hc0s, hc0r, hc1s, hc1r, zss, zur, zdr, oss, orr):
    p, y, a = lax.axis_index("cz"), lax.axis_index("cy"), lax.axis_index("cx")
    core, ax = lax.rem(a, 2), a // 2
    rows, half = 16 * 4, w1s.shape[1]
    a_c, a_x, a_d = a + 1 - 2 * core, lax.rem(a + 2, 4), 3 - a
    a_d = lax.rem(a_c + 2, 4)
    ypeer, cpeer, xpeer = {"cy": 1 - y}, {"cx": a_c}, {"cx": a_x}
    up, down = {"cz": lax.rem(p + 1, 4)}, {"cz": lax.rem(p + 3, 4)}
    spot = 2 * core + ax
    mine, theirs = 2 * core, 2 - 2 * core

    def rcopy(src, dst, ss, rs, device):
        return pltpu.make_async_remote_copy(
            src_ref=src, dst_ref=dst, send_sem=ss, recv_sem=rs, device_id=device, device_id_type=MESH)

    def lanes(owner, width):
        return pl.ds(pl.multiple_of(owner * half, 128), width)

    loads = [
        pltpu.make_async_copy(x_ref, xb.at[pl.ds(4 * p, 4), spot], wsem.at[0]),
        pltpu.make_async_copy(w1_ref.at[:, lanes(1 - y, half)], w1s, wsem.at[1]),
        pltpu.make_async_copy(w1_ref.at[:, lanes(y, half)], w1o, wsem.at[2]),
        pltpu.make_async_copy(w2_ref, w2, wsem.at[3]),
    ]
    for load in loads:
        load.start()

    barrier = pltpu.get_barrier_semaphore()
    for device in (ypeer, cpeer, xpeer, {"cx": a_d}):
        pl.semaphore_signal(barrier, inc=1, device_id=device, device_id_type=MESH)

    @pl.when(p < 3)
    def _():
        pl.semaphore_signal(barrier, inc=1, device_id=up, device_id_type=MESH)

    @pl.when(p > 0)
    def _():
        pl.semaphore_signal(barrier, inc=1, device_id=down, device_id_type=MESH)

    @pl.when((p == 0) | (p == 3))
    def _():
        pl.semaphore_wait(barrier, 5)

    @pl.when((p > 0) & (p < 3))
    def _():
        pl.semaphore_wait(barrier, 6)

    def own_to_x(j):
        piece = xb.at[4 * p + j, spot]
        return rcopy(piece, piece, xxs.at[j], xxr.at[j], xpeer)

    def own_to_core(j):
        piece = xb.at[4 * p + j, spot]
        return rcopy(piece, piece, xc0s.at[j], xcr.at[4 * p + j], cpeer)

    def passed_to_core(j):
        piece = xb.at[4 * p + j, 2 * core + 1 - ax]
        return rcopy(piece, piece, xc1s.at[j], xcr.at[4 * p + j], cpeer)

    def x_up(g):
        pair = xb.at[g, pl.ds(mine, 2)]
        return rcopy(pair, pair, xus.at[g], xzr.at[g], up)

    def x_down(g):
        pair = xb.at[g, pl.ds(mine, 2)]
        return rcopy(pair, pair, xds.at[g], xzr.at[g], down)

    def pair_to_core(g):
        pair = xb.at[g, pl.ds(mine, 2)]
        return rcopy(pair, pair, xc2s.at[g], xcr.at[g], cpeer)

    def own_arrived(j):
        piece = xb.at[4 * p + j, 2 * core + 1 - ax]
        rcopy(piece, piece, xxs.at[j], xxr.at[j], xpeer).wait_recv()
        passed_to_core(j).start()

        @pl.when(p < 3)
        def _():
            x_up(4 * p + j).start()

        @pl.when(p > 0)
        def _():
            x_down(4 * p + j).start()

    loads[0].wait()
    for j in range(4):
        own_to_x(j).start()
        own_to_core(j).start()
    own_arrived(0)
    loads[1].wait()
    loads[2].wait()

    def chunk(i):
        q, j = (i + 2) // 4 - 1, lax.rem(i + 2, 4)
        other = jnp.where(p < 2, 1 + q, 2 - q)
        other = jnp.where((p == 1) & (q == 0), 0, other)
        other = jnp.where((p == 2) & (q == 0), 3, other)
        first, last = i < 2, i >= 14
        block = jnp.where(first | last, p, other)
        return 4 * block + jnp.where(first, i, jnp.where(last, i - 12, j))

    def c_send(g):
        return rcopy(cs.at[g], cr.at[g], css, crr.at[g], ypeer)

    def h_piece(g, owner, width):
        return hb.at[g, :, lanes(owner, width)]

    def layer1(g):
        theirs_x = xb.at[g, pl.ds(theirs, 2)]
        rcopy(theirs_x, theirs_x, xc2s.at[g], xcr.at[g], cpeer).wait_recv()
        xv = xb[g].reshape(rows, xb.shape[3])
        cs[g] = jnp.dot(xv, w1s[...], preferred_element_type=jnp.float32)
        c_send(g).start()
        co[g] = jnp.dot(xv, w1o[...], preferred_element_type=jnp.float32)

    def h_to_y(g):
        piece = h_piece(g, 2 * a + y, half)
        return rcopy(piece, piece, hys, hyr.at[g], ypeer)

    def h_to_x(g):
        piece = h_piece(g, 2 * a + y, half)
        return rcopy(piece, piece, hx0s, hx0r.at[g], xpeer)

    def hy_to_x(g):
        piece = h_piece(g, 2 * a + 1 - y, half)
        return rcopy(piece, piece, hx1s, hx1r.at[g], xpeer)

    def h_to_core(g):
        piece = h_piece(g, 2 * a, 2 * half)
        return rcopy(piece, piece, hc0s, hc0r.at[g], cpeer)

    def hx_to_core(g):
        piece = h_piece(g, 2 * a_x, 2 * half)
        return rcopy(piece, piece, hc1s, hc1r.at[g], cpeer)

    def activation(g):
        rcopy(cr.at[g], cr.at[g], css, crr.at[g], ypeer).wait_recv()
        c = (co[g] + cr[g]).astype(jnp.bfloat16).astype(jnp.float32)
        h = jax.nn.gelu(c, approximate=True).astype(jnp.bfloat16)
        hb[g, :, lanes(2 * a + y, half)] = h
        h_to_y(g).start()
        h_to_x(g).start()

    def pass_y(g):
        piece = h_piece(g, 2 * a + 1 - y, half)
        rcopy(piece, piece, hys, hyr.at[g], ypeer).wait_recv()
        hy_to_x(g).start()
        h_to_core(g).start()

    def pass_x(g):
        piece = h_piece(g, 2 * a_x + y, half)
        rcopy(piece, piece, hx0s, hx0r.at[g], xpeer).wait_recv()
        piece = h_piece(g, 2 * a_x + 1 - y, half)
        rcopy(piece, piece, hx1s, hx1r.at[g], xpeer).wait_recv()
        hx_to_core(g).start()

    def layer2(g):
        piece = h_piece(g, 2 * a_c, 2 * half)
        rcopy(piece, piece, hc0s, hc0r.at[g], cpeer).wait_recv()
        piece = h_piece(g, 2 * a_d, 2 * half)
        rcopy(piece, piece, hc1s, hc1r.at[g], cpeer).wait_recv()
        zp[g] = jnp.dot(hb[g], w2[...], preferred_element_type=jnp.float32)

    def z_up(g):
        return rcopy(zp.at[g], zu.at[g], zss.at[g], zur.at[g], up)

    def z_down(g):
        return rcopy(zp.at[g], zd.at[g], zss.at[g], zdr.at[g], down)

    def from_below(g):
        rcopy(zu.at[g], zu.at[g], zss.at[g], zur.at[g], up).wait_recv()

    def from_above(g):
        rcopy(zd.at[g], zd.at[g], zss.at[g], zdr.at[g], down).wait_recv()

    def below_to_up(g):
        from_below(g)
        zp[g] = zp[g] + zu[g]
        z_up(g).start()

    def above_to_down(g):
        from_above(g)
        zp[g] = zp[g] + zd[g]
        z_down(g).start()

    def out_copy(j, e):
        owner = (a_c, a_x, a_d)[e]
        q = 2 * lax.rem(owner, 2) + owner // 2
        return rcopy(ob.at[j, q], o_ref.at[j, :, lanes(a, half)], oss, orr, {"cx": owner})

    def out_own(j):
        return pltpu.make_async_copy(ob.at[j, spot], o_ref.at[j, :, lanes(a, half)], orr)

    def finish(j):
        g = 4 * p + j

        @pl.when(p > 0)
        def _():
            from_below(g)
            zp[g] = zp[g] + zu[g]

        @pl.when(p < 3)
        def _():
            from_above(g)
            zp[g] = zp[g] + zd[g]

        ob[j] = zp[g].astype(jnp.bfloat16).reshape(ob.shape[1:])
        for e in range(3):
            out_copy(j, e).start()
        out_own(j).start()

    edge = (p == 0) | (p == 3)

    def step(s, carry):
        @pl.when(s < 16)
        def _():
            layer1(chunk(s))

        @pl.when((s >= LH) & (s < 16 + LH))
        def _():
            activation(chunk(s - LH))

        @pl.when(s < 3)
        def _():
            own_arrived(s + 1)

        d, jz = (s + 3) // 4, lax.rem(s + 3, 4)

        @pl.when((s >= 1) & (s <= 12) & (p - d >= 0))
        def _():
            g = 4 * (p - d) + jz
            pair = xb.at[g, pl.ds(mine, 2)]
            rcopy(pair, pair, xus.at[g], xzr.at[g], up).wait_recv()

            @pl.when(p < 3)
            def _():
                x_up(g).start()

            pair_to_core(g).start()

        @pl.when((s >= 1) & (s <= 12) & (p + d <= 3))
        def _():
            g = 4 * (p + d) + jz
            pair = xb.at[g, pl.ds(mine, 2)]
            rcopy(pair, pair, xds.at[g], xzr.at[g], down).wait_recv()

            @pl.when(p > 0)
            def _():
                x_down(g).start()

            pair_to_core(g).start()

        t = s - L2

        @pl.when(t == 0)
        def _():
            loads[3].wait()

        @pl.when((t >= 0) & (t < 16))
        def _():
            layer2(chunk(t))

        @pl.when((t >= 2) & (t < 14) & (p == 0))
        def _():
            z_up(chunk(t)).start()

        @pl.when((t >= 2) & (t < 14) & (p == 3))
        def _():
            z_down(chunk(t)).start()

        @pl.when((t >= 7) & (t < 15) & (p == 1))
        def _():
            below_to_up(chunk(t - 1))

        @pl.when((t >= 7) & (t < 15) & (p == 2))
        def _():
            above_to_down(chunk(t - 1))

        @pl.when((t >= 12) & (t < 16) & (p == 1))
        def _():
            above_to_down(chunk(t - 10))

        @pl.when((t >= 12) & (t < 16) & (p == 2))
        def _():
            below_to_up(chunk(t - 10))

        @pl.when((s >= LF) & (s < 16 + LF))
        def _():
            pass_y(chunk(s - LF))

        @pl.when((s >= LC) & (s < 16 + LC))
        def _():
            pass_x(chunk(s - LC))

        @pl.when(t >= 13)
        def _():
            finish(t - 13)

        return carry

    lax.fori_loop(0, STEPS, step, 0)

    rcopy(o_ref, o_ref, oss, orr, cpeer).wait_recv()
    rcopy(ob.at[:, pl.ds(0, 3)], ob.at[:, pl.ds(0, 3)], oss, orr, cpeer).wait_send()
    rcopy(cs, cs, css, crr.at[0], cpeer).wait_send()
    one = hb.at[:, :, pl.ds(0, half)]
    two = hb.at[:, :, pl.ds(0, 2 * half)]
    rcopy(one, one, hys, hyr.at[0], cpeer).wait_send()
    rcopy(one, one, hx0s, hx0r.at[0], cpeer).wait_send()
    rcopy(one, one, hx1s, hx1r.at[0], cpeer).wait_send()
    rcopy(two, two, hc0s, hc0r.at[0], cpeer).wait_send()
    rcopy(two, two, hc1s, hc1r.at[0], cpeer).wait_send()

    def drain(g, carry):
        block = g // 4

        @pl.when(block == p)
        def _():
            j = lax.rem(g, 4)
            own_to_x(j).wait_send()
            own_to_core(j).wait_send()
            passed_to_core(j).wait_send()

        @pl.when(block != p)
        def _():
            pair_to_core(g).wait_send()
            z_up(g).wait_send()

        @pl.when((block <= p) & (p < 3))
        def _():
            x_up(g).wait_send()

        @pl.when((block >= p) & (p > 0))
        def _():
            x_down(g).wait_send()

        return carry

    lax.fori_loop(0, 16, drain, 0)


def solution(mesh):
    def body(x, w1, w2):
        r, d = x.shape
        k1, n1 = w1.shape
        k2, n2 = w2.shape
        half = n1 // 2
        f32, bf16 = jnp.float32, jnp.bfloat16
        dma = pltpu.SemaphoreType.DMA
        out = pl.pallas_call(
            kernel,
            out_shape=jax.ShapeDtypeStruct((4, r // 4, d), bf16),
            in_specs=[pl.BlockSpec(memory_space=pl.ANY)] * 3,
            out_specs=pl.BlockSpec(memory_space=pl.ANY),
            scratch_shapes=[
                pltpu.VMEM((k1, half), bf16),
                pltpu.VMEM((k1, half), bf16),
                pltpu.VMEM((k2, n2), bf16),
                pltpu.VMEM((16, 4, 16, d), bf16),
                pltpu.VMEM((16, 64, half), f32),
                pltpu.VMEM((16, 64, half), f32),
                pltpu.VMEM((16, 64, half), f32),
                pltpu.VMEM((16, 64, k2), bf16),
                pltpu.VMEM((16, 64, n2), f32),
                pltpu.VMEM((16, 64, n2), f32),
                pltpu.VMEM((16, 64, n2), f32),
                pltpu.VMEM((4, 4, 16, n2), bf16),
                dma((4,)),
                dma((4,)), dma((4,)),
                dma((16,)), dma((16,)), dma((16,)),
                dma((4,)), dma((4,)), dma((16,)), dma((16,)),
                dma(()), dma((16,)),
                dma(()), dma((16,)),
                dma(()), dma((16,)),
                dma(()), dma((16,)),
                dma(()), dma((16,)),
                dma(()), dma((16,)),
                dma((16,)), dma((16,)), dma((16,)),
                dma(()), dma(()),
            ],
            compiler_params=pltpu.CompilerParams(
                collective_id=0, has_side_effects=True, vmem_limit_bytes=60 * 1024 * 1024),
            name="mlp",
        )(x.reshape(4, r // 4, d), w1, w2)
        return out.reshape(r, d)

    return jax.shard_map(
        body,
        mesh=mesh,
        in_specs=(P(("cx", "cz"), "cy"), P("cy", ("cz", "cx")), P("cz", ("cy", "cx"))),
        out_specs=P(("cx", "cz"), "cy"),
        check_vma=False,
    )
```

time: 564 us -> 121 us (0.21)
  waiting for transfers between devices: 517 us -> 0 us
  Pallas kernels: 0 us -> 119 us
  matrix products: 27.7 us -> 0 us
  between operations: 13.5 us -> 0.01 us
    all_gather x4 -> x0, waiting for transfers between devices: 397 us -> none  [the longest x1 162 us: body(): w1g = lax.all_gather(w1, 'cx', axis=1, tiled=True)]
    pallas_call x0 -> x1, Pallas kernels: none -> 119 us  [body(): pl.pallas_call(kernel, out_shape=jax.ShapeDtypeStruct((4, r // 4, d), bf1...]
    reduce_scatter x2 -> x0, waiting for transfers between devices: 118 us -> none  [the longest x1 65.2 us: body(): lax.psum_scatter(cp, 'cy', scatter_dimension=0, tiled=True)]
    dot_general x2 -> x0, matrix products: 27.7 us -> none  [the longest x1 13.9 us: body(): cp = jnp.dot(xg, w1g, preferred_element_type=jnp.float32)]
  transfers between devices with their start and end apart: 6 -> 0, of which waited for: 6 -> 0; matrix products, arithmetic and copies ran while one was open for 1% -> 0% of each run, Pallas kernels for 0% -> 0%
where the time goes in v1:
time: 121 us
  Pallas kernels  119 us (98%)
  local copies, waits for them, and re-layouts  1.72 us (1%)
    pallas_call x1, Pallas kernels, body(): pl.pallas_call(kernel, out_shape=jax.ShapeDtypeStruct((4, r // 4, d), bf1...  119 us

profile of v1, /device:TPU:0, one launch (start us, length us, event | category | flops | bytes accessed | tf_op | source)
XLA Modules:
  0.0 121.0 jit_solution(4503751080247678349)
XLA Ops:
  0.0 119.3 %mlp.1 = bf16[4,16,2560]{2,1,0:T(8,128)(2,1)} custom-call(bf16[4,16,2560]{2,1,0:T(8,128)(2,1)} %bitcast.3, bf16[2560,1280]{1,0:T(8,128)(2,1)} %w1_ref.1, bf16[5120,640]{1,0:T(8,128)(2,1)} %w2_ref.1), custom_call_target="tpu_custom_call" | custom-call | tf_op jit(solution)/shard_map/mlp/pallas_call | solution.py:366
  119.3 1.7 %copy.5 = bf16[64,2560]{1,0:T(8,128)(2,1)} copy(bf16[64,2560]{1,0:T(8,128)(2,1)} %bitcast.2) | data formatting | bytes 655360

commit v2 on v0

v2 whole, which is shorter than its diff:
```python
import jax
import jax.numpy as jnp
from jax import lax
from jax.experimental import pallas as pl
from jax.experimental.pallas import tpu as pltpu
from jax.sharding import PartitionSpec as P

MESH = pl.DeviceIdType.MESH
CHUNKS, ROWS = 32, 32
LH, LF, LC, L2 = 2, 4, 5, 7
LZ = 2
EDGE = (0, 2, 4, 5, 6, 7, 3, 1)
MIDDLE = (2, 0, 1, 4, 6, 7, 5, 3)
X_EDGE = ((3, 1, 0), (5, 1, 1), (7, 2, 0), (8, 2, 1), (10, 2, 2), (11, 2, 3), (12, 3, 0), (14, 3, 1), (15, 3, 2), (17, 3, 3),
          (18, 1, 2), (20, 1, 3))
X_BACK = ((3, 0, 0), (5, 0, 1), (6, 0, 2), (8, 0, 3))
X_FRONT = ((3, 2, 0), (5, 2, 1), (6, 2, 2), (8, 2, 3), (9, 3, 0), (11, 3, 1), (12, 3, 2), (14, 3, 3))
X_LATE = ((12, 1, 2), (14, 1, 3))


def pick(index, pairs, default=0):
    value = jnp.int32(default)
    for key, item in pairs:
        value = jnp.where(index == key, jnp.int32(item), value)
    return value


def kernel(x_ref, w1_ref, w2_ref, o_ref, w1s, w1o, w2, xb, cs, co, cr, hb, zp, zf, zb, ob,
           wsem, xxs, xxr, xfs, xbs, xzr, xc0s, xc0r, xc1s, xc1r, xc2s, xc2r, css, crr, hys, hyr, hx0s, hx0r, hx1s, hx1r,
           hc0s, hc0r, hc1s, hc1r, zss, zfr, zbr, oss, orr):
    p, y, a = lax.axis_index("cz"), lax.axis_index("cy"), lax.axis_index("cx")
    core, ax = lax.rem(a, 2), a // 2
    half = w1s.shape[1]
    a_c, a_x = a + 1 - 2 * core, lax.rem(a + 2, 4)
    a_d = lax.rem(a_c + 2, 4)
    low = p < 2
    edge = (p == 0) | (p == 3)
    middle = (p > 0) & (p < 3)
    ypeer, cpeer, xpeer, dpeer = {"cy": 1 - y}, {"cx": a_c}, {"cx": a_x}, {"cx": a_d}
    front = {"cz": jnp.where(low, p + 1, p - 1)}
    back = {"cz": jnp.where(edge, p, jnp.where(low, p - 1, p + 1))}

    def rcopy(src, dst, ss, rs, device):
        return pltpu.make_async_remote_copy(
            src_ref=src, dst_ref=dst, send_sem=ss, recv_sem=rs, device_id=device, device_id_type=MESH)

    def arrived(ref, sem):
        rcopy(ref, ref, oss, sem, cpeer).wait_recv()

    def sent(ref, sem):
        rcopy(ref, ref, sem, orr, cpeer).wait_send()

    def lanes(owner, width):
        return pl.ds(pl.multiple_of(owner * half, 128), width)

    def plane(k):
        return jnp.where(low, k, 3 - k)

    loads = [
        pltpu.make_async_copy(x_ref, xb.at[pl.ds(4 * p, 4), ax, core], wsem.at[0]),
        pltpu.make_async_copy(w1_ref.at[:, lanes(1 - y, half)], w1s, wsem.at[1]),
        pltpu.make_async_copy(w1_ref.at[:, lanes(y, half)], w1o, wsem.at[2]),
        pltpu.make_async_copy(w2_ref, w2, wsem.at[3]),
    ]
    for load in loads:
        load.start()

    barrier = pltpu.get_barrier_semaphore()
    for device in (ypeer, cpeer, xpeer, dpeer, front):
        pl.semaphore_signal(barrier, inc=1, device_id=device, device_id_type=MESH)

    @pl.when(middle)
    def _():
        pl.semaphore_signal(barrier, inc=1, device_id=back, device_id_type=MESH)
        pl.semaphore_wait(barrier, 6)

    @pl.when(edge)
    def _():
        pl.semaphore_wait(barrier, 5)

    def x_front(g):
        pair = xb.at[g, :, core]
        rcopy(pair, pair, xfs, xzr.at[g], front).start()

    def x_back(g):
        pair = xb.at[g, :, core]
        rcopy(pair, pair, xbs, xzr.at[g], back).start()

    def pair_to_core(g):
        pair = xb.at[g, :, core]
        rcopy(pair, pair, xc2s, xc2r.at[g], cpeer).start()

    def own_arrived(j):
        piece = xb.at[4 * p + j, 1 - ax, core]
        arrived(piece, xxr.at[j])
        rcopy(piece, piece, xc1s, xc1r.at[j], cpeer).start()
        x_front(4 * p + j)

        @pl.when(middle & (j < 2))
        def _():
            x_back(4 * p + j)

    loads[0].wait()
    for j in range(4):
        piece = xb.at[4 * p + j, ax, core]
        rcopy(piece, piece, xc0s, xc0r.at[j], cpeer).start()
        rcopy(piece, piece, xxs, xxr.at[j], xpeer).start()
    loads[1].wait()

    def chunk(i):
        place = i // 4
        base = jnp.where(edge, pick(place, tuple(enumerate(EDGE))), pick(place, tuple(enumerate(MIDDLE))))
        return 8 * plane(base // 2) + 4 * lax.rem(base, 2) + lax.rem(i, 4)

    def chunk1(i):
        turn = i // 2
        first = 8 * p + 2 * lax.rem(i, 2) + turn + ax - 2 * turn * ax
        return jnp.where(i < 4, first, chunk(i))

    def layer1(n):
        g, h = n // 2, lax.rem(n, 2)
        j = lax.rem(g, 4)
        own = g // 4 == p
        theirs = xb.at[g, :, 1 - core]

        @pl.when(own & (h == ax))
        def _():
            arrived(xb.at[g, h, 1 - core], xc0r.at[j])

        @pl.when(own & (h != ax))
        def _():
            arrived(xb.at[g, h, 1 - core], xc1r.at[j])

        @pl.when((g // 4 != p) & (h == 0))
        def _():
            arrived(theirs, xc2r.at[g])

        xv = xb[g, h].reshape(ROWS, xb.shape[4])
        cs[n] = jnp.dot(xv, w1s[...], preferred_element_type=jnp.float32)
        rcopy(cs.at[n], cr.at[n], css, crr.at[n], ypeer).start()

        @pl.when(n == 8 * p + ax)
        def _():
            loads[2].wait()

        co[n] = jnp.dot(xv, w1o[...], preferred_element_type=jnp.float32)

    def h_piece(n, owner, width):
        return hb.at[n, :, lanes(owner, width)]

    def activation(n):
        arrived(cr.at[n], crr.at[n])
        c = (co[n] + cr[n]).astype(jnp.bfloat16).astype(jnp.float32)
        hb[n, :, lanes(2 * a + y, half)] = jax.nn.gelu(c, approximate=True).astype(jnp.bfloat16)
        piece = h_piece(n, 2 * a + y, half)
        rcopy(piece, piece, hys, hyr.at[n], ypeer).start()
        rcopy(piece, piece, hx0s, hx0r.at[n], xpeer).start()

    def pass_y(n):
        piece = h_piece(n, 2 * a + 1 - y, half)
        arrived(piece, hyr.at[n])
        rcopy(piece, piece, hx1s, hx1r.at[n], xpeer).start()
        piece = h_piece(n, 2 * a, 2 * half)
        rcopy(piece, piece, hc0s, hc0r.at[n], cpeer).start()

    def pass_x(n):
        arrived(h_piece(n, 2 * a_x + y, half), hx0r.at[n])
        arrived(h_piece(n, 2 * a_x + 1 - y, half), hx1r.at[n])
        piece = h_piece(n, 2 * a_x, 2 * half)
        rcopy(piece, piece, hc1s, hc1r.at[n], cpeer).start()

    def layer2(n):
        arrived(h_piece(n, 2 * a_c, 2 * half), hc0r.at[n])
        arrived(h_piece(n, 2 * a_d, 2 * half), hc1r.at[n])
        zp[n] = jnp.dot(hb[n], w2[...], preferred_element_type=jnp.float32)

    def from_front(n):
        arrived(zf.at[n], zfr.at[n])
        zp[n] = zp[n] + zf[n]

    def from_back(n):
        arrived(zb.at[n], zbr.at[n])
        zp[n] = zp[n] + zb[n]

    def finish(i):
        n = 8 * p + i
        from_front(n)

        @pl.when(middle)
        def _():
            from_back(n)

        ob[i] = zp[n].astype(jnp.bfloat16).reshape(ob.shape[1:])
        j, h = i // 2, lax.rem(i, 2)
        place = o_ref.at[j, :, lanes(a, half)]

        @pl.when(h == ax)
        def _():
            pltpu.make_async_copy(ob.at[i, core], place, orr).start()
            rcopy(ob.at[i, 1 - core], place, oss, orr, cpeer).start()

        @pl.when(h != ax)
        def _():
            rcopy(ob.at[i, core], place, oss, orr, xpeer).start()
            rcopy(ob.at[i, 1 - core], place, oss, orr, dpeer).start()

    def step(s, carry):
        @pl.when(s < CHUNKS)
        def _():
            layer1(chunk1(s))

        @pl.when((s >= LH) & (s < CHUNKS + LH))
        def _():
            activation(chunk1(s - LH))

        @pl.when(s == 1)
        def _():
            own_arrived(0)

        @pl.when((s >= 1) & (s < 4))
        def _():
            own_arrived(s)

        group = pick(s, [(at, 4 * k + j) for at, k, j in X_EDGE], -1)

        @pl.when(edge & (group >= 0))
        def _():
            g = 4 * plane(group // 4) + lax.rem(group, 4)
            arrived(xb.at[g, :, core], xzr.at[g])
            pair_to_core(g)

        group_b = pick(s, [(at, 4 * k + j) for at, k, j in X_BACK], -1)

        @pl.when(middle & (group_b >= 0))
        def _():
            g = 4 * plane(group_b // 4) + lax.rem(group_b, 4)
            arrived(xb.at[g, :, core], xzr.at[g])
            x_front(g)
            pair_to_core(g)

        group_f = pick(s, [(at, 4 * k + j) for at, k, j in X_FRONT], -1)

        @pl.when(middle & (group_f >= 0))
        def _():
            g = 4 * plane(group_f // 4) + lax.rem(group_f, 4)
            arrived(xb.at[g, :, core], xzr.at[g])
            x_back(g)
            pair_to_core(g)

        late = pick(s, [(at, j) for at, _, j in X_LATE], -1)

        @pl.when(middle & (late >= 0))
        def _():
            x_back(4 * p + late)

        t = s - L2

        @pl.when(t == 0)
        def _():
            loads[3].wait()

        @pl.when((t >= 0) & (t < CHUNKS))
        def _():
            layer2(chunk(t))

        def z_front(n, to):
            rcopy(zp.at[n], to.at[n], zss, (zbr if to is zb else zfr).at[n], front).start()

        @pl.when(edge & (t >= 4) & (t < 28))
        def _():
            z_front(chunk(t), zb)

        @pl.when(middle & (((t >= 12) & (t < 16)) | ((t >= 24) & (t < 28))))
        def _():
            n = chunk(t)
            from_back(n)
            z_front(n, zf)

        @pl.when(middle & (t >= 16 + LZ) & (t < 24 + LZ))
        def _():
            n = chunk(t - LZ)
            from_back(n)
            z_front(n, zf)

        @pl.when(middle & (t >= 16 + 2 * LZ) & (t < 24 + 2 * LZ))
        def _():
            n = chunk(t - 12 - 2 * LZ)
            from_front(n)
            rcopy(zp.at[n], zf.at[n], zss, zfr.at[n], back).start()

        @pl.when((s >= LF) & (s < CHUNKS + LF))
        def _():
            pass_y(chunk1(s - LF))

        @pl.when((s >= LC) & (s < CHUNKS + LC))
        def _():
            pass_x(chunk(s - LC))

        @pl.when(t >= 24)
        def _():
            finish(t - 24)

        return carry

    lax.fori_loop(0, CHUNKS + L2, step, 0)

    arrived(o_ref, orr)
    sent(ob.at[pl.ds(0, 6)], oss)
    sent(cs, css)
    for sem in (hys, hx0s, hx1s):
        sent(hb.at[:, :, pl.ds(0, half)], sem)
    for sem in (hc0s, hc1s):
        sent(hb.at[:, :, pl.ds(0, 2 * half)], sem)
    sent(zp.at[pl.ds(0, 24)], zss)
    for sem in (xxs, xc0s, xc1s):
        sent(xb.at[pl.ds(0, 4), 0, 0], sem)
    sent(xb.at[pl.ds(0, 12), :, 0], xc2s)

    @pl.when(edge)
    def _():
        sent(xb.at[pl.ds(0, 4), :, 0], xfs)

    @pl.when(middle)
    def _():
        sent(xb.at[pl.ds(0, 8), :, 0], xfs)
        sent(xb.at[pl.ds(0, 12), :, 0], xbs)


def solution(mesh):
    def body(x, w1, w2):
        r, d = x.shape
        k1, n1 = w1.shape
        k2, n2 = w2.shape
        half = n1 // 2
        f32, bf16 = jnp.float32, jnp.bfloat16
        dma = pltpu.SemaphoreType.DMA
        one, four, groups, chunks = dma(()), dma((4,)), dma((16,)), dma((CHUNKS,))
        out = pl.pallas_call(
            kernel,
            out_shape=jax.ShapeDtypeStruct((4, r // 4, d), bf16),
            in_specs=[pl.BlockSpec(memory_space=pl.ANY)] * 3,
            out_specs=pl.BlockSpec(memory_space=pl.ANY),
            scratch_shapes=[
                pltpu.VMEM((k1, half), bf16),
                pltpu.VMEM((k1, half), bf16),
                pltpu.VMEM((k2, n2), bf16),
                pltpu.VMEM((16, 2, 2, 16, d), bf16),
                pltpu.VMEM((CHUNKS, ROWS, half), f32),
                pltpu.VMEM((CHUNKS, ROWS, half), f32),
                pltpu.VMEM((CHUNKS, ROWS, half), f32),
                pltpu.VMEM((CHUNKS, ROWS, k2), bf16),
                pltpu.VMEM((CHUNKS, ROWS, n2), f32),
                pltpu.VMEM((CHUNKS, ROWS, n2), f32),
                pltpu.VMEM((CHUNKS, ROWS, n2), f32),
                pltpu.VMEM((8, 2, 16, n2), bf16),
                four,
                one, four,
                one, one, groups,
                one, four, one, four, one, groups,
                one, chunks,
                one, chunks,
                one, chunks,
                one, chunks,
                one, chunks,
                one, chunks,
                one, chunks, chunks,
                one, one,
            ],
            compiler_params=pltpu.CompilerParams(
                collective_id=0, has_side_effects=True, vmem_limit_bytes=60 * 1024 * 1024),
            name="mlp",
        )(x.reshape(4, r // 4, d), w1, w2)
        return out.reshape(r, d)

    return jax.shard_map(
        body,
        mesh=mesh,
        in_specs=(P(("cx", "cz"), "cy"), P("cy", ("cz", "cx")), P("cz", ("cy", "cx"))),
        out_specs=P(("cx", "cz"), "cy"),
        check_vma=False,
    )
```

time: 564 us -> 129 us (0.23)
  waiting for transfers between devices: 517 us -> 0 us
  Pallas kernels: 0 us -> 125 us
  matrix products: 27.7 us -> 0 us
  between operations: 13.5 us -> 0.01 us
    all_gather x4 -> x0, waiting for transfers between devices: 397 us -> none  [the longest x1 162 us: body(): w1g = lax.all_gather(w1, 'cx', axis=1, tiled=True)]
    pallas_call x0 -> x1, Pallas kernels: none -> 125 us  [body(): pl.pallas_call(kernel, out_shape=jax.ShapeDtypeStruct((4, r // 4, d), bf1...]
    reduce_scatter x2 -> x0, waiting for transfers between devices: 118 us -> none  [the longest x1 65.2 us: body(): lax.psum_scatter(cp, 'cy', scatter_dimension=0, tiled=True)]
    dot_general x2 -> x0, matrix products: 27.7 us -> none  [the longest x1 13.9 us: body(): cp = jnp.dot(xg, w1g, preferred_element_type=jnp.float32)]
  transfers between devices with their start and end apart: 6 -> 0, of which waited for: 6 -> 0; matrix products, arithmetic and copies ran while one was open for 1% -> 0% of each run, Pallas kernels for 0% -> 0%
where the time goes in v2:
time: 129 us; the launch traced here: 127 us
  Pallas kernels  125 us (97%)
  local copies, waits for them, and re-layouts  1.72 us (1%)
    pallas_call x1, Pallas kernels, body(): pl.pallas_call(kernel, out_shape=jax.ShapeDtypeStruct((4, r // 4, d), bf1...  125 us

profile of v2, /device:TPU:0, one launch (start us, length us, event | category | flops | bytes accessed | tf_op | source)
XLA Modules:
  0.0 127.2 jit_solution(4564061982032764488)
XLA Ops:
  0.0 125.5 %mlp.1 = bf16[4,16,2560]{2,1,0:T(8,128)(2,1)} custom-call(bf16[4,16,2560]{2,1,0:T(8,128)(2,1)} %bitcast.3, bf16[2560,1280]{1,0:T(8,128)(2,1)} %w1_ref.1, bf16[5120,640]{1,0:T(8,128)(2,1)} %w2_ref.1), custom_call_target="tpu_custom_call" | custom-call | tf_op jit(solution)/shard_map/mlp/pallas_call | solution.py:338
  125.5 1.7 %copy.5 = bf16[64,2560]{1,0:T(8,128)(2,1)} copy(bf16[64,2560]{1,0:T(8,128)(2,1)} %bitcast.2) | data formatting | bytes 655360

commit v3 on v2

--- a/solution.py
+++ b/solution.py
@@ -7,15 +7,15 @@
 
 MESH = pl.DeviceIdType.MESH
 CHUNKS, ROWS = 32, 32
-LH, LF, LC, L2 = 2, 4, 5, 7
-LZ = 2
-EDGE = (0, 2, 4, 5, 6, 7, 3, 1)
+TURNS = 20
+LH, LF, LC, L2 = 2, 4, 5, 6
+EDGE = (0, 2, 4, 6, 7, 5, 3, 1)
 MIDDLE = (2, 0, 1, 4, 6, 7, 5, 3)
-X_EDGE = ((3, 1, 0), (5, 1, 1), (7, 2, 0), (8, 2, 1), (10, 2, 2), (11, 2, 3), (12, 3, 0), (14, 3, 1), (15, 3, 2), (17, 3, 3),
-          (18, 1, 2), (20, 1, 3))
-X_BACK = ((3, 0, 0), (5, 0, 1), (6, 0, 2), (8, 0, 3))
-X_FRONT = ((3, 2, 0), (5, 2, 1), (6, 2, 2), (8, 2, 3), (9, 3, 0), (11, 3, 1), (12, 3, 2), (14, 3, 3))
-X_LATE = ((12, 1, 2), (14, 1, 3))
+X_EDGE = tuple((3 + e, k, j) for e, (k, j) in enumerate(
+    ((1, 0), (1, 1), (2, 0), (2, 1), (3, 0), (3, 1), (3, 2), (3, 3), (2, 2), (2, 3), (1, 2), (1, 3))))
+X_BACK = tuple((3 + j, 0, j) for j in range(4))
+X_FRONT = tuple((3 + e, 2 + e // 4, e % 4) for e in range(8))
+X_LATE = ((10, 1, 2), (11, 1, 3))
 
 
 def pick(index, pairs, default=0):
@@ -26,8 +26,8 @@
 
 
 def kernel(x_ref, w1_ref, w2_ref, o_ref, w1s, w1o, w2, xb, cs, co, cr, hb, zp, zf, zb, ob,
-           wsem, xxs, xxr, xfs, xbs, xzr, xc0s, xc0r, xc1s, xc1r, xc2s, xc2r, css, crr, hys, hyr, hx0s, hx0r, hx1s, hx1r,
-           hc0s, hc0r, hc1s, hc1r, zss, zfr, zbr, oss, orr):
+           wsem, xxs, xxr, xfs, xbs, xzr, xc0s, xc0r, xc1s, xc1r, xc2s, xc2r, css, crr, hys, hyr, hxs, hxr,
+           hcs, hcr, zss, zfr, zbr, oss, orr):
     p, y, a = lax.axis_index("cz"), lax.axis_index("cy"), lax.axis_index("cx")
     core, ax = lax.rem(a, 2), a // 2
     half = w1s.shape[1]
@@ -107,111 +107,125 @@
         rcopy(piece, piece, xxs, xxr.at[j], xpeer).start()
     loads[1].wait()
 
-    def chunk(i):
-        place = i // 4
+    def chunk(u):
+        place = (u - 2) // 2
         base = jnp.where(edge, pick(place, tuple(enumerate(EDGE))), pick(place, tuple(enumerate(MIDDLE))))
-        return 8 * plane(base // 2) + 4 * lax.rem(base, 2) + lax.rem(i, 4)
-
-    def chunk1(i):
-        turn = i // 2
-        first = 8 * p + 2 * lax.rem(i, 2) + turn + ax - 2 * turn * ax
-        return jnp.where(i < 4, first, chunk(i))
-
-    def layer1(n):
+        other = 8 * plane(base // 2) + 4 * lax.rem(base, 2) + 2 * lax.rem(u, 2)
+        return jnp.where(u < 4, 8 * p + u, jnp.where(u < 16, other, 8 * p + u - 12))
+
+    def chunk1(u):
+        turn = u // 2
+        first = 8 * p + 2 * lax.rem(u, 2) + turn + ax - 2 * turn * ax
+        return jnp.where(u < 4, first, chunk(u))
+
+    def rows_of(ref, n, count):
+        return ref.at[pl.ds(n, count)]
+
+    def product(xv, w, count):
+        z = jnp.dot(xv.reshape(count * ROWS, xv.shape[-1]), w[...], preferred_element_type=jnp.float32)
+        return z.reshape(count, ROWS, z.shape[1])
+
+    def layer1(n, count, start):
         g, h = n // 2, lax.rem(n, 2)
-        j = lax.rem(g, 4)
-        own = g // 4 == p
-        theirs = xb.at[g, :, 1 - core]
-
-        @pl.when(own & (h == ax))
-        def _():
-            arrived(xb.at[g, h, 1 - core], xc0r.at[j])
-
-        @pl.when(own & (h != ax))
-        def _():
-            arrived(xb.at[g, h, 1 - core], xc1r.at[j])
-
-        @pl.when((g // 4 != p) & (h == 0))
-        def _():
-            arrived(theirs, xc2r.at[g])
-
-        xv = xb[g, h].reshape(ROWS, xb.shape[4])
-        cs[n] = jnp.dot(xv, w1s[...], preferred_element_type=jnp.float32)
-        rcopy(cs.at[n], cr.at[n], css, crr.at[n], ypeer).start()
-
-        @pl.when(n == 8 * p + ax)
-        def _():
-            loads[2].wait()
-
-        co[n] = jnp.dot(xv, w1o[...], preferred_element_type=jnp.float32)
-
-    def h_piece(n, owner, width):
-        return hb.at[n, :, lanes(owner, width)]
-
-    def activation(n):
-        arrived(cr.at[n], crr.at[n])
-        c = (co[n] + cr[n]).astype(jnp.bfloat16).astype(jnp.float32)
-        hb[n, :, lanes(2 * a + y, half)] = jax.nn.gelu(c, approximate=True).astype(jnp.bfloat16)
-        piece = h_piece(n, 2 * a + y, half)
+        if count == 2:
+            arrived(xb.at[g, :, 1 - core], xc2r.at[g])
+            xv = xb[g]
+        else:
+            j = lax.rem(g, 4)
+
+            @pl.when(h == ax)
+            def _():
+                arrived(xb.at[g, h, 1 - core], xc0r.at[j])
+
+            @pl.when(h != ax)
+            def _():
+                arrived(xb.at[g, h, 1 - core], xc1r.at[j])
+
+            xv = xb[g, h]
+        cs[pl.ds(n, count)] = product(xv, w1s, count)
+        rcopy(rows_of(cs, n, count), rows_of(cr, n, count), css, crr.at[n], ypeer).start()
+        if count == 1:
+            @pl.when(start)
+            def _():
+                loads[2].wait()
+
+        co[pl.ds(n, count)] = product(xv, w1o, count)
+
+    def h_piece(n, count, owner, width):
+        return hb.at[pl.ds(n, count), :, lanes(owner, width)]
+
+    def activation(n, count):
+        arrived(rows_of(cr, n, count), crr.at[n])
+        c = (co[pl.ds(n, count)] + cr[pl.ds(n, count)]).astype(jnp.bfloat16).astype(jnp.float32)
+        h = jax.nn.gelu(c, approximate=True).astype(jnp.bfloat16)
+        hb[pl.ds(n, count), :, lanes(2 * a + y, half)] = h
+        piece = h_piece(n, count, 2 * a + y, half)
         rcopy(piece, piece, hys, hyr.at[n], ypeer).start()
-        rcopy(piece, piece, hx0s, hx0r.at[n], xpeer).start()
-
-    def pass_y(n):
-        piece = h_piece(n, 2 * a + 1 - y, half)
+        rcopy(piece, piece, hxs, hxr.at[n], xpeer).start()
+
+    def pass_y(n, count):
+        piece = h_piece(n, count, 2 * a + 1 - y, half)
         arrived(piece, hyr.at[n])
-        rcopy(piece, piece, hx1s, hx1r.at[n], xpeer).start()
-        piece = h_piece(n, 2 * a, 2 * half)
-        rcopy(piece, piece, hc0s, hc0r.at[n], cpeer).start()
-
-    def pass_x(n):
-        arrived(h_piece(n, 2 * a_x + y, half), hx0r.at[n])
-        arrived(h_piece(n, 2 * a_x + 1 - y, half), hx1r.at[n])
-        piece = h_piece(n, 2 * a_x, 2 * half)
-        rcopy(piece, piece, hc1s, hc1r.at[n], cpeer).start()
-
-    def layer2(n):
-        arrived(h_piece(n, 2 * a_c, 2 * half), hc0r.at[n])
-        arrived(h_piece(n, 2 * a_d, 2 * half), hc1r.at[n])
-        zp[n] = jnp.dot(hb[n], w2[...], preferred_element_type=jnp.float32)
-
-    def from_front(n):
-        arrived(zf.at[n], zfr.at[n])
-        zp[n] = zp[n] + zf[n]
-
-    def from_back(n):
-        arrived(zb.at[n], zbr.at[n])
-        zp[n] = zp[n] + zb[n]
-
-    def finish(i):
+        rcopy(piece, piece, hxs, hxr.at[n], xpeer).start()
+        piece = h_piece(n, count, 2 * a, 2 * half)
+        rcopy(piece, piece, hcs, hcr.at[n], cpeer).start()
+
+    def pass_x(n, count):
+        piece = h_piece(n, count, 2 * a_x, 2 * half)
+        arrived(piece, hxr.at[n])
+        rcopy(piece, piece, hcs, hcr.at[n], cpeer).start()
+
+    def layer2(n, count):
+        arrived(h_piece(n, count, 0, 4 * half), hcr.at[n])
+        zp[pl.ds(n, count)] = product(hb[pl.ds(n, count)], w2, count)
+
+    def z_send(n, to, sems, device):
+        rcopy(rows_of(zp, n, 2), rows_of(to, n, 2), zss, sems.at[n], device).start()
+
+    def add(n, count, ref):
+        zp[pl.ds(n, count)] = zp[pl.ds(n, count)] + ref[pl.ds(n, count)]
+
+    def out_piece(i, c, j, device):
+        rcopy(ob.at[i, c], o_ref.at[j, :, lanes(a, half)], oss, orr, device).start()
+
+    def out_own(i, j):
+        pltpu.make_async_copy(ob.at[i, core], o_ref.at[j, :, lanes(a, half)], orr).start()
+        out_piece(i, 1 - core, j, cpeer)
+
+    def out_other(i, j):
+        out_piece(i, core, j, xpeer)
+        out_piece(i, 1 - core, j, dpeer)
+
+    def partials_arrived(n):
+        arrived(rows_of(zf, n, 2), zfr.at[n])
+
+        @pl.when(middle)
+        def _():
+            arrived(rows_of(zb, n, 2), zbr.at[n])
+
+    def finish(i, count):
         n = 8 * p + i
-        from_front(n)
+        add(n, count, zf)
 
         @pl.when(middle)
         def _():
-            from_back(n)
-
-        ob[i] = zp[n].astype(jnp.bfloat16).reshape(ob.shape[1:])
-        j, h = i // 2, lax.rem(i, 2)
-        place = o_ref.at[j, :, lanes(a, half)]
-
-        @pl.when(h == ax)
-        def _():
-            pltpu.make_async_copy(ob.at[i, core], place, orr).start()
-            rcopy(ob.at[i, 1 - core], place, oss, orr, cpeer).start()
-
-        @pl.when(h != ax)
-        def _():
-            rcopy(ob.at[i, core], place, oss, orr, xpeer).start()
-            rcopy(ob.at[i, 1 - core], place, oss, orr, dpeer).start()
+            add(n, count, zb)
+
+        ob[pl.ds(i, count)] = zp[pl.ds(n, count)].astype(jnp.bfloat16).reshape((count,) + ob.shape[1:])
 
     def step(s, carry):
-        @pl.when(s < CHUNKS)
-        def _():
-            layer1(chunk1(s))
-
-        @pl.when((s >= LH) & (s < CHUNKS + LH))
-        def _():
-            activation(chunk1(s - LH))
+        def each(u, event):
+            @pl.when(((u >= 0) & (u < 4)) | ((u >= 16) & (u < TURNS)))
+            def _():
+                event(u, 1)
+
+            @pl.when((u >= 4) & (u < 16))
+            def _():
+                event(u, 2)
+
+        each(s, lambda u, count: layer1(chunk1(u), count, s == 0))
+        each(s - LH, lambda u, count: activation(chunk1(u), count))
+        each(s - LF, lambda u, count: pass_y(chunk1(u), count))
 
         @pl.when(s == 1)
         def _():
@@ -259,58 +273,64 @@
         def _():
             loads[3].wait()
 
-        @pl.when((t >= 0) & (t < CHUNKS))
-        def _():
-            layer2(chunk(t))
-
-        def z_front(n, to):
-            rcopy(zp.at[n], to.at[n], zss, (zbr if to is zb else zfr).at[n], front).start()
-
-        @pl.when(edge & (t >= 4) & (t < 28))
-        def _():
-            z_front(chunk(t), zb)
-
-        @pl.when(middle & (((t >= 12) & (t < 16)) | ((t >= 24) & (t < 28))))
+        each(t, lambda u, count: layer2(chunk(u), count))
+
+        @pl.when(edge & (t >= 4) & (t < 16))
+        def _():
+            z_send(chunk(t), zb, zbr, front)
+
+        @pl.when(middle & (t >= 8) & (t < 16))
         def _():
             n = chunk(t)
-            from_back(n)
-            z_front(n, zf)
-
-        @pl.when(middle & (t >= 16 + LZ) & (t < 24 + LZ))
-        def _():
-            n = chunk(t - LZ)
-            from_back(n)
-            z_front(n, zf)
-
-        @pl.when(middle & (t >= 16 + 2 * LZ) & (t < 24 + 2 * LZ))
-        def _():
-            n = chunk(t - 12 - 2 * LZ)
-            from_front(n)
-            rcopy(zp.at[n], zf.at[n], zss, zfr.at[n], back).start()
-
-        @pl.when((s >= LF) & (s < CHUNKS + LF))
-        def _():
-            pass_y(chunk1(s - LF))
-
-        @pl.when((s >= LC) & (s < CHUNKS + LC))
-        def _():
-            pass_x(chunk(s - LC))
-
-        @pl.when(t >= 24)
-        def _():
-            finish(t - 24)
+            arrived(rows_of(zb, n, 2), zbr.at[n])
+            add(n, 2, zb)
+            z_send(n, zf, zfr, front)
+
+        @pl.when(middle & (t >= 12) & (t < 16))
+        def _():
+            n = 8 * plane(0) + 2 * (t - 12)
+            arrived(rows_of(zf, n, 2), zfr.at[n])
+            add(n, 2, zf)
+            z_send(n, zf, zfr, back)
+
+        each(s - LC, lambda u, count: pass_x(chunk(u), count))
+
+        @pl.when((t >= 15) & (t < 17))
+        def _():
+            j = t - 15
+            partials_arrived(8 * p + 2 * j)
+            finish(2 * j, 2)
+            out_own(2 * j + ax, j)
+            out_other(2 * j + 1 - ax, j)
+
+        @pl.when(t >= 16)
+        def _():
+            i = t - 12
+            j, h = i // 2, lax.rem(i, 2)
+
+            @pl.when(h == 0)
+            def _():
+                partials_arrived(8 * p + i)
+
+            finish(i, 1)
+
+            @pl.when(h == ax)
+            def _():
+                out_own(i, j)
+
+            @pl.when(h != ax)
+            def _():
+                out_other(i, j)
 
         return carry
 
-    lax.fori_loop(0, CHUNKS + L2, step, 0)
+    lax.fori_loop(0, TURNS + L2, step, 0)
 
     arrived(o_ref, orr)
     sent(ob.at[pl.ds(0, 6)], oss)
     sent(cs, css)
-    for sem in (hys, hx0s, hx1s):
-        sent(hb.at[:, :, pl.ds(0, half)], sem)
-    for sem in (hc0s, hc1s):
-        sent(hb.at[:, :, pl.ds(0, 2 * half)], sem)
+    for sem, width in ((hys, half), (hxs, 2 * half), (hcs, 4 * half)):
+        sent(hb.at[:, :, pl.ds(0, width)], sem)
     sent(zp.at[pl.ds(0, 24)], zss)
     for sem in (xxs, xc0s, xc1s):
         sent(xb.at[pl.ds(0, 4), 0, 0], sem)
@@ -361,8 +381,6 @@
                 one, chunks,
                 one, chunks,
                 one, chunks,
-                one, chunks,
-                one, chunks,
                 one, chunks, chunks,
                 one, one,
             ],

time: 129 us -> 117 us (0.907)
  Pallas kernels: 125 us -> 114 us
    pallas_call x1, Pallas kernels: 125 us -> 114 us  [body(): pl.pallas_call(kernel, out_shape=jax.ShapeDtypeStruct((4, r // 4, d), bf1...]
where the time goes in v3:
time: 117 us; the launch traced here: 115 us
  Pallas kernels  114 us (97%)
  local copies, waits for them, and re-layouts  1.72 us (1%)
    pallas_call x1, Pallas kernels, body(): pl.pallas_call(kernel, out_shape=jax.ShapeDtypeStruct((4, r // 4, d), bf1...  114 us

profile of v3, /device:TPU:0, one launch (start us, length us, event | category | flops | bytes accessed | tf_op | source)
XLA Modules:
  0.0 115.3 jit_solution(16684908569580127094)
XLA Ops:
  0.0 113.5 %mlp.1 = bf16[4,16,2560]{2,1,0:T(8,128)(2,1)} custom-call(bf16[4,16,2560]{2,1,0:T(8,128)(2,1)} %bitcast.3, bf16[2560,1280]{1,0:T(8,128)(2,1)} %w1_ref.1, bf16[5120,640]{1,0:T(8,128)(2,1)} %w2_ref.1), custom_call_target="tpu_custom_call" | custom-call | tf_op jit(solution)/shard_map/mlp/pallas_call | solution.py:358
  113.5 1.7 %copy.5 = bf16[64,2560]{1,0:T(8,128)(2,1)} copy(bf16[64,2560]{1,0:T(8,128)(2,1)} %bitcast.2) | data formatting | bytes 655360

commit v4 on v3

--- a/solution.py
+++ b/solution.py
@@ -8,7 +8,7 @@
 MESH = pl.DeviceIdType.MESH
 CHUNKS, ROWS = 32, 32
 TURNS = 20
-LH, LF, LC, L2 = 2, 4, 5, 6
+LH, LF, LC, L2 = 1, 3, 5, 6
 EDGE = (0, 2, 4, 6, 7, 5, 3, 1)
 MIDDLE = (2, 0, 1, 4, 6, 7, 5, 3)
 X_EDGE = tuple((3 + e, k, j) for e, (k, j) in enumerate(
@@ -224,7 +224,6 @@
                 event(u, 2)
 
         each(s, lambda u, count: layer1(chunk1(u), count, s == 0))
-        each(s - LH, lambda u, count: activation(chunk1(u), count))
         each(s - LF, lambda u, count: pass_y(chunk1(u), count))
 
         @pl.when(s == 1)
@@ -267,6 +266,8 @@
         def _():
             x_back(4 * p + late)
 
+        each(s - LC, lambda u, count: pass_x(chunk(u), count))
+
         t = s - L2
 
         @pl.when(t == 0)
@@ -293,7 +294,7 @@
             add(n, 2, zf)
             z_send(n, zf, zfr, back)
 
-        each(s - LC, lambda u, count: pass_x(chunk(u), count))
+        each(s - LH, lambda u, count: activation(chunk1(u), count))
 
         @pl.when((t >= 15) & (t < 17))
         def _():

time: 117 us -> 110 us (0.940)
  Pallas kernels: 114 us -> 107 us
    pallas_call x1, Pallas kernels: 114 us -> 107 us  [body(): pl.pallas_call(kernel, out_shape=jax.ShapeDtypeStruct((4, r // 4, d), bf1...]
where the time goes in v4:
time: 110 us; the launch traced here: 109 us
  Pallas kernels  107 us (97%)
  local copies, waits for them, and re-layouts  1.72 us (2%)
    pallas_call x1, Pallas kernels, body(): pl.pallas_call(kernel, out_shape=jax.ShapeDtypeStruct((4, r // 4, d), bf1...  107 us

profile of v4, /device:TPU:0, one launch (start us, length us, event | category | flops | bytes accessed | tf_op | source)
XLA Modules:
  0.0 108.9 jit_solution(18091224225894100165)
XLA Ops:
  0.0 107.2 %mlp.1 = bf16[4,16,2560]{2,1,0:T(8,128)(2,1)} custom-call(bf16[4,16,2560]{2,1,0:T(8,128)(2,1)} %bitcast.3, bf16[2560,1280]{1,0:T(8,128)(2,1)} %w1_ref.1, bf16[5120,640]{1,0:T(8,128)(2,1)} %w2_ref.1), custom_call_target="tpu_custom_call" | custom-call | tf_op jit(solution)/shard_map/mlp/pallas_call | solution.py:359
  107.2 1.7 %copy.5 = bf16[64,2560]{1,0:T(8,128)(2,1)} copy(bf16[64,2560]{1,0:T(8,128)(2,1)} %bitcast.2) | data formatting | bytes 655360

commit v5 on v4

--- a/solution.py
+++ b/solution.py
@@ -7,8 +7,13 @@
 
 MESH = pl.DeviceIdType.MESH
 CHUNKS, ROWS = 32, 32
-TURNS = 20
+LOOPED = 16
 LH, LF, LC, L2 = 1, 3, 5, 6
+TAIL = (
+    "L10 C11 F13 C12 Z10 M16 L11 Z11 F14 C13 H15 L12 Z12 H16 B0 M18 C14 B1 H17 L13 Z13 F15 L14 F16 B2 H18 Z14 H19 C15 "
+    "F17 F18 C16 B3 L15 Z15 F19 C17 O0 C18 O1 L16 C19 O2 L18 O3")
+
+
 EDGE = (0, 2, 4, 6, 7, 5, 3, 1)
 MIDDLE = (2, 0, 1, 4, 6, 7, 5, 3)
 X_EDGE = tuple((3 + e, k, j) for e, (k, j) in enumerate(
@@ -57,10 +62,11 @@
         return jnp.where(low, k, 3 - k)
 
     loads = [
-        pltpu.make_async_copy(x_ref, xb.at[pl.ds(4 * p, 4), ax, core], wsem.at[0]),
-        pltpu.make_async_copy(w1_ref.at[:, lanes(1 - y, half)], w1s, wsem.at[1]),
-        pltpu.make_async_copy(w1_ref.at[:, lanes(y, half)], w1o, wsem.at[2]),
-        pltpu.make_async_copy(w2_ref, w2, wsem.at[3]),
+        pltpu.make_async_copy(x_ref.at[pl.ds(16 * j, 16)], xb.at[4 * p + j, ax, core], wsem.at[j]) for j in range(4)]
+    loads += [
+        pltpu.make_async_copy(w1_ref.at[:, lanes(1 - y, half)], w1s, wsem.at[4]),
+        pltpu.make_async_copy(w1_ref.at[:, lanes(y, half)], w1o, wsem.at[5]),
+        pltpu.make_async_copy(w2_ref, w2, wsem.at[6]),
     ]
     for load in loads:
         load.start()
@@ -100,12 +106,12 @@
         def _():
             x_back(4 * p + j)
 
-    loads[0].wait()
     for j in range(4):
         piece = xb.at[4 * p + j, ax, core]
+        loads[j].wait()
         rcopy(piece, piece, xc0s, xc0r.at[j], cpeer).start()
         rcopy(piece, piece, xxs, xxr.at[j], xpeer).start()
-    loads[1].wait()
+    loads[4].wait()
 
     def chunk(u):
         place = (u - 2) // 2
@@ -147,9 +153,18 @@
         if count == 1:
             @pl.when(start)
             def _():
-                loads[2].wait()
+                loads[5].wait()
 
         co[pl.ds(n, count)] = product(xv, w1o, count)
+
+    def layer1_last(n, j):
+        arrived(xb.at[4 * p + j, ax, 1 - core], xc0r.at[j])
+        arrived(xb.at[4 * p + j, 1 - ax, 1 - core], xc1r.at[j])
+        xv = xb[4 * p + j]
+        cs[pl.ds(n, 2)] = product(xv, w1s, 2)
+        for i in range(2):
+            rcopy(rows_of(cs, n + i, 1), rows_of(cr, n + i, 1), css, crr.at[n + i], ypeer).start()
+        co[pl.ds(n, 2)] = product(xv, w1o, 2)
 
     def h_piece(n, count, owner, width):
         return hb.at[pl.ds(n, count), :, lanes(owner, width)]
@@ -175,9 +190,23 @@
         arrived(piece, hxr.at[n])
         rcopy(piece, piece, hcs, hcr.at[n], cpeer).start()
 
-    def layer2(n, count):
-        arrived(h_piece(n, count, 0, 4 * half), hcr.at[n])
-        zp[pl.ds(n, count)] = product(hb[pl.ds(n, count)], w2, count)
+    def layer2(n, own):
+        if own is None:
+            arrived(h_piece(n, 2, 0, 4 * half), hcr.at[n])
+        elif own is True:
+            arrived(h_piece(n, 1, 0, 4 * half), hcr.at[n])
+            arrived(h_piece(n + 1, 1, 0, 4 * half), hcr.at[n + 1])
+        else:
+            @pl.when(own)
+            def _():
+                arrived(h_piece(n, 1, 0, 4 * half), hcr.at[n])
+                arrived(h_piece(n + 1, 1, 0, 4 * half), hcr.at[n + 1])
+
+            @pl.when(jnp.logical_not(own))
+            def _():
+                arrived(h_piece(n, 2, 0, 4 * half), hcr.at[n])
+
+        zp[pl.ds(n, 2)] = product(hb[pl.ds(n, 2)], w2, 2)
 
     def z_send(n, to, sems, device):
         rcopy(rows_of(zp, n, 2), rows_of(to, n, 2), zss, sems.at[n], device).start()
@@ -203,23 +232,39 @@
         def _():
             arrived(rows_of(zb, n, 2), zbr.at[n])
 
-    def finish(i, count):
-        n = 8 * p + i
-        add(n, count, zf)
+    def finish(j):
+        n = 8 * p + 2 * j
+        partials_arrived(n)
+        add(n, 2, zf)
 
         @pl.when(middle)
         def _():
-            add(n, count, zb)
-
-        ob[pl.ds(i, count)] = zp[pl.ds(n, count)].astype(jnp.bfloat16).reshape((count,) + ob.shape[1:])
+            add(n, 2, zb)
+
+        ob[pl.ds(2 * j, 2)] = zp[pl.ds(n, 2)].astype(jnp.bfloat16).reshape((2,) + ob.shape[1:])
+        out_other(2 * j + 1 - ax, j)
+        out_own(2 * j + ax, j)
+
+    def z_edge(n):
+        z_send(n, zb, zbr, front)
+
+    def z_middle(n):
+        arrived(rows_of(zb, n, 2), zbr.at[n])
+        add(n, 2, zb)
+        z_send(n, zf, zfr, front)
+
+    def z_back(n):
+        arrived(rows_of(zf, n, 2), zfr.at[n])
+        add(n, 2, zf)
+        z_send(n, zf, zfr, back)
 
     def step(s, carry):
         def each(u, event):
-            @pl.when(((u >= 0) & (u < 4)) | ((u >= 16) & (u < TURNS)))
+            @pl.when((u >= 0) & (u < 4))
             def _():
                 event(u, 1)
 
-            @pl.when((u >= 4) & (u < 16))
+            @pl.when(u >= 4)
             def _():
                 event(u, 2)
 
@@ -270,62 +315,49 @@
 
         t = s - L2
 
-        @pl.when(t == 0)
-        def _():
-            loads[3].wait()
-
-        each(t, lambda u, count: layer2(chunk(u), count))
-
-        @pl.when(edge & (t >= 4) & (t < 16))
-        def _():
-            z_send(chunk(t), zb, zbr, front)
-
-        @pl.when(middle & (t >= 8) & (t < 16))
-        def _():
-            n = chunk(t)
-            arrived(rows_of(zb, n, 2), zbr.at[n])
-            add(n, 2, zb)
-            z_send(n, zf, zfr, front)
-
-        @pl.when(middle & (t >= 12) & (t < 16))
-        def _():
-            n = 8 * plane(0) + 2 * (t - 12)
-            arrived(rows_of(zf, n, 2), zfr.at[n])
-            add(n, 2, zf)
-            z_send(n, zf, zfr, back)
+        @pl.when(t == 1)
+        def _():
+            loads[6].wait()
+
+        @pl.when((t == 1) | (t >= 3))
+        def _():
+            layer2(chunk(jnp.where(t < 4, t - 1, t)), t < 4)
+
+        @pl.when(edge & (t >= 4))
+        def _():
+            z_edge(chunk(t))
+
+        @pl.when(middle & (t >= 8))
+        def _():
+            z_middle(chunk(t))
 
         each(s - LH, lambda u, count: activation(chunk1(u), count))
-
-        @pl.when((t >= 15) & (t < 17))
-        def _():
-            j = t - 15
-            partials_arrived(8 * p + 2 * j)
-            finish(2 * j, 2)
-            out_own(2 * j + ax, j)
-            out_other(2 * j + 1 - ax, j)
-
-        @pl.when(t >= 16)
-        def _():
-            i = t - 12
-            j, h = i // 2, lax.rem(i, 2)
-
-            @pl.when(h == 0)
-            def _():
-                partials_arrived(8 * p + i)
-
-            finish(i, 1)
-
-            @pl.when(h == ax)
-            def _():
-                out_own(i, j)
-
-            @pl.when(h != ax)
-            def _():
-                out_other(i, j)
-
         return carry
 
-    lax.fori_loop(0, TURNS + L2, step, 0)
+    lax.fori_loop(0, LOOPED, step, 0)
+
+    def tail(kind, u):
+        n, count = chunk(jnp.int32(u)), 2 if u < 16 else 1
+        if kind == "M":
+            layer1_last(n, 2 + (u - 16) // 2)
+        elif kind == "H":
+            activation(n, count)
+        elif kind == "F":
+            pass_y(n, count)
+        elif kind == "C":
+            pass_x(n, count)
+        elif kind == "L":
+            layer2(n, None if u < 16 else True)
+        elif kind == "Z":
+            pl.when(edge)(lambda: z_edge(n))
+            pl.when(middle)(lambda: z_middle(n))
+        elif kind == "B":
+            pl.when(middle)(lambda: z_back(8 * plane(0) + 2 * u))
+        elif kind == "O":
+            finish(u)
+
+    for event in TAIL.split():
+        tail(event[0], int(event[1:]))
 
     arrived(o_ref, orr)
     sent(ob.at[pl.ds(0, 6)], oss)
@@ -359,7 +391,7 @@
         out = pl.pallas_call(
             kernel,
             out_shape=jax.ShapeDtypeStruct((4, r // 4, d), bf16),
-            in_specs=[pl.BlockSpec(memory_space=pl.ANY)] * 3,
+            in_specs=[pl.BlockSpec(memory_space=pltpu.HBM)] * 3,
             out_specs=pl.BlockSpec(memory_space=pl.ANY),
             scratch_shapes=[
                 pltpu.VMEM((k1, half), bf16),
@@ -374,7 +406,7 @@
                 pltpu.VMEM((CHUNKS, ROWS, n2), f32),
                 pltpu.VMEM((CHUNKS, ROWS, n2), f32),
                 pltpu.VMEM((8, 2, 16, n2), bf16),
-                four,
+                dma((7,)),
                 one, four,
                 one, one, groups,
                 one, four, one, four, one, groups,
@@ -386,9 +418,9 @@
                 one, one,
             ],
             compiler_params=pltpu.CompilerParams(
-                collective_id=0, has_side_effects=True, vmem_limit_bytes=60 * 1024 * 1024),
+                collective_id=0, has_side_effects=True, vmem_limit_bytes=48 * 1024 * 1024),
             name="mlp",
-        )(x.reshape(4, r // 4, d), w1, w2)
+        )(x, w1, w2)
         return out.reshape(r, d)
 
     return jax.shard_map(

time: 110 us -> 108 us (0.982); the launches traced: 109 us -> 108 us
  no operation moved by 1% of the time
where the time goes in v5:
time: 108 us
  Pallas kernels  106 us (98%)
  local copies, waits for them, and re-layouts  1.7 us (2%)
    pallas_call x1, Pallas kernels, body(): pl.pallas_call(kernel, out_shape=jax.ShapeDtypeStruct((4, r // 4, d), bf1...  106 us

profile of v5, /device:TPU:0, one launch (start us, length us, event | category | flops | bytes accessed | tf_op | source)
XLA Modules:
  0.0 108.1 jit_solution(12065738757744402037)
XLA Ops:
  0.0 0.0 copy-start
  0.0 1.0 copy-done
  1.0 106.4 %mlp.1 = bf16[4,16,2560]{2,1,0:T(8,128)(2,1)S(1)} custom-call(bf16[64,2560]{1,0:T(8,128)(2,1)S(1)} %copy-done, bf16[2560,1280]{1,0:T(8,128)(2,1)} %w1_ref.1, bf16[5120,640]{1,0:T(8,128)(2,1)} %w2_ref.1), custom_call_target="tpu_custom_call" | custom-call | tf_op jit(solution)/shard_map/mlp/pallas_call | solution.py:391
  107.3 0.7 copy.5
Async XLA Ops:
  0.0 1.0 copy-start

commit v6 on v5

--- a/solution.py
+++ b/solution.py
@@ -10,17 +10,21 @@
 LOOPED = 16
 LH, LF, LC, L2 = 1, 3, 5, 6
 TAIL = (
-    "L10 C11 F13 C12 Z10 M16 L11 Z11 F14 C13 H15 L12 Z12 H16 B0 M18 C14 B1 H17 L13 Z13 F15 L14 F16 B2 H18 Z14 H19 C15 "
-    "F17 F18 C16 B3 L15 Z15 F19 C17 O0 C18 O1 L16 C19 O2 L18 O3")
-
-
+    ("L", 10), ("F", 13), ("Z", 10), ("C", 11), ("M", 16), ("L", 11), ("H", 15), ("C", 12), ("Z", 11), ("C", 13),
+    ("M", 18), ("F", 14), ("L", 12), ("H", 16), ("B", 0), ("Z", 12), ("L", 13), ("H", 17), ("C", 14), ("B", 1),
+    ("F", 15), ("Z", 13), ("L", 14), ("H", 18), ("Z", 14), ("B", 2), ("H", 19), ("F", 16), ("C", 15), ("F", 17),
+    ("F", 18), ("L", 15), ("Z", 15), ("B", 3), ("F", 19), ("O", 0), ("C", 16), ("C", 17), ("O", 1), ("C", 18),
+    ("L", 16), ("C", 19), ("O", 2), ("L", 18), ("O", 3),
+)
 EDGE = (0, 2, 4, 6, 7, 5, 3, 1)
 MIDDLE = (2, 0, 1, 4, 6, 7, 5, 3)
 X_EDGE = tuple((3 + e, k, j) for e, (k, j) in enumerate(
     ((1, 0), (1, 1), (2, 0), (2, 1), (3, 0), (3, 1), (3, 2), (3, 3), (2, 2), (2, 3), (1, 2), (1, 3))))
 X_BACK = tuple((3 + j, 0, j) for j in range(4))
-X_FRONT = tuple((3 + e, 2 + e // 4, e % 4) for e in range(8))
-X_LATE = ((10, 1, 2), (11, 1, 3))
+X_FRONT = tuple((3 + e, k, j) for e, (k, j) in enumerate(
+    ((2, 0), (2, 1), (3, 0), (3, 1), (3, 2), (3, 3), (2, 2), (2, 3))))
+X_LATE_FRONT = ((7, 2), (8, 3))
+X_LATE_BACK = ((10, 2), (11, 3))
 
 
 def pick(index, pairs, default=0):
@@ -100,7 +104,10 @@
         piece = xb.at[4 * p + j, 1 - ax, core]
         arrived(piece, xxr.at[j])
         rcopy(piece, piece, xc1s, xc1r.at[j], cpeer).start()
-        x_front(4 * p + j)
+
+        @pl.when(edge | (j < 2))
+        def _():
+            x_front(4 * p + j)
 
         @pl.when(middle & (j < 2))
         def _():
@@ -271,13 +278,9 @@
         each(s, lambda u, count: layer1(chunk1(u), count, s == 0))
         each(s - LF, lambda u, count: pass_y(chunk1(u), count))
 
-        @pl.when(s == 1)
-        def _():
-            own_arrived(0)
-
-        @pl.when((s >= 1) & (s < 4))
-        def _():
-            own_arrived(s)
+        @pl.when((s >= 1) & (s < 5))
+        def _():
+            own_arrived(s - 1)
 
         group = pick(s, [(at, 4 * k + j) for at, k, j in X_EDGE], -1)
 
@@ -305,11 +308,12 @@
             x_back(g)
             pair_to_core(g)
 
-        late = pick(s, [(at, j) for at, _, j in X_LATE], -1)
-
-        @pl.when(middle & (late >= 0))
-        def _():
-            x_back(4 * p + late)
+        for order, send in ((X_LATE_FRONT, x_front), (X_LATE_BACK, x_back)):
+            late = pick(s, order, -1)
+
+            @pl.when(middle & (late >= 0))
+            def _():
+                send(4 * p + late)
 
         each(s - LC, lambda u, count: pass_x(chunk(u), count))
 
@@ -356,8 +360,8 @@
         elif kind == "O":
             finish(u)
 
-    for event in TAIL.split():
-        tail(event[0], int(event[1:]))
+    for kind, u in TAIL:
+        tail(kind, u)
 
     arrived(o_ref, orr)
     sent(ob.at[pl.ds(0, 6)], oss)
@@ -420,7 +424,7 @@
             compiler_params=pltpu.CompilerParams(
                 collective_id=0, has_side_effects=True, vmem_limit_bytes=48 * 1024 * 1024),
             name="mlp",
-        )(x, w1, w2)
+        )(pltpu.with_memory_space_constraint(x, pltpu.HBM), w1, w2)
         return out.reshape(r, d)
 
     return jax.shard_map(

time: 108 us -> 105 us (0.972)
  Pallas kernels: 106 us -> 104 us
    pallas_call x1, Pallas kernels: 106 us -> 104 us  [body(): pl.pallas_call(kernel, out_shape=jax.ShapeDtypeStruct((4, r // 4, d), bf1...]
where the time goes in v6:
time: 105 us; the launch traced here: 104 us
  Pallas kernels  104 us (99%)
    pallas_call x1, Pallas kernels, body(): pl.pallas_call(kernel, out_shape=jax.ShapeDtypeStruct((4, r // 4, d), bf1...  104 us

profile of v6, /device:TPU:0, one launch (start us, length us, event | category | flops | bytes accessed | tf_op | source)
XLA Modules:
  0.0 104.4 jit_solution(9762082053678126525)
XLA Ops:
  0.0 103.7 %mlp.1 = bf16[4,16,2560]{2,1,0:T(8,128)(2,1)S(1)} custom-call(bf16[64,2560]{1,0:T(8,128)(2,1)} %x_ref.1, bf16[2560,1280]{1,0:T(8,128)(2,1)} %w1_ref.1, bf16[5120,640]{1,0:T(8,128)(2,1)} %w2_ref.1), custom_call_target="tpu_custom_call" | custom-call | tf_op jit(solution)/shard_map/mlp/pallas_call | solution.py:395
  103.7 0.7 copy.5

commit v7 on v6

--- a/solution.py
+++ b/solution.py
@@ -72,7 +72,7 @@
         pltpu.make_async_copy(w1_ref.at[:, lanes(y, half)], w1o, wsem.at[5]),
         pltpu.make_async_copy(w2_ref, w2, wsem.at[6]),
     ]
-    for load in loads:
+    for load in loads[:6]:
         load.start()
 
     barrier = pltpu.get_barrier_semaphore()
@@ -96,6 +96,14 @@
         pair = xb.at[g, :, core]
         rcopy(pair, pair, xbs, xzr.at[g], back).start()
 
+    def x_part(j, owner):
+        part = xb.at[4 * p + j, owner, core]
+        rcopy(part, part, xfs, xzr.at[4 * p + j], front).start()
+
+        @pl.when(middle)
+        def _():
+            rcopy(part, part, xbs, xzr.at[4 * p + j], back).start()
+
     def pair_to_core(g):
         pair = xb.at[g, :, core]
         rcopy(pair, pair, xc2s, xc2r.at[g], cpeer).start()
@@ -105,20 +113,24 @@
         arrived(piece, xxr.at[j])
         rcopy(piece, piece, xc1s, xc1r.at[j], cpeer).start()
 
-        @pl.when(edge | (j < 2))
+        @pl.when(j < 2)
+        def _():
+            x_part(j, 1 - ax)
+
+        @pl.when(edge & (j >= 2))
         def _():
             x_front(4 * p + j)
-
-        @pl.when(middle & (j < 2))
-        def _():
-            x_back(4 * p + j)
 
     for j in range(4):
         piece = xb.at[4 * p + j, ax, core]
         loads[j].wait()
         rcopy(piece, piece, xc0s, xc0r.at[j], cpeer).start()
         rcopy(piece, piece, xxs, xxr.at[j], xpeer).start()
+        if j < 2:
+            x_part(j, ax)
+
     loads[4].wait()
+    loads[6].start()
 
     def chunk(u):
         place = (u - 2) // 2
@@ -143,9 +155,18 @@
         if count == 2:
             arrived(xb.at[g, :, 1 - core], xc2r.at[g])
             xv = xb[g]
+            cs[pl.ds(n, count)] = product(xv, w1s, count)
+            rcopy(rows_of(cs, n, count), rows_of(cr, n, count), css, crr.at[n], ypeer).start()
         else:
             j = lax.rem(g, 4)
 
+            def part(c):
+                rows = pl.ds(pl.multiple_of(16 * c, 16), 16)
+                cs[n, rows] = jnp.dot(xb[g, h, c], w1s[...], preferred_element_type=jnp.float32)
+                rcopy(cs.at[n, rows], cr.at[n, rows], css, crr.at[n], ypeer).start()
+
+            part(core)
+
             @pl.when(h == ax)
             def _():
                 arrived(xb.at[g, h, 1 - core], xc0r.at[j])
@@ -154,10 +175,9 @@
             def _():
                 arrived(xb.at[g, h, 1 - core], xc1r.at[j])
 
+            part(1 - core)
             xv = xb[g, h]
-        cs[pl.ds(n, count)] = product(xv, w1s, count)
-        rcopy(rows_of(cs, n, count), rows_of(cr, n, count), css, crr.at[n], ypeer).start()
-        if count == 1:
+
             @pl.when(start)
             def _():
                 loads[5].wait()

time: 105 us -> 104 us (level)
  no operation moved by 1% of the time
where the time goes in v7:
time: 104 us
  Pallas kernels  103 us (99%)
    pallas_call x1, Pallas kernels, body(): pl.pallas_call(kernel, out_shape=jax.ShapeDtypeStruct((4, r // 4, d), bf1...  103 us

profile of v7, /device:TPU:0, one launch (start us, length us, event | category | flops | bytes accessed | tf_op | source)
XLA Modules:
  0.0 104.0 jit_solution(9550292034245231803)
XLA Ops:
  0.0 103.3 %mlp.1 = bf16[4,16,2560]{2,1,0:T(8,128)(2,1)S(1)} custom-call(bf16[64,2560]{1,0:T(8,128)(2,1)} %x_ref.1, bf16[2560,1280]{1,0:T(8,128)(2,1)} %w1_ref.1, bf16[5120,640]{1,0:T(8,128)(2,1)} %w2_ref.1), custom_call_target="tpu_custom_call" | custom-call | tf_op jit(solution)/shard_map/mlp/pallas_call | solution.py:415
  103.3 0.7 copy.5

commit v8 on v7

--- a/solution.py
+++ b/solution.py
@@ -72,7 +72,7 @@
         pltpu.make_async_copy(w1_ref.at[:, lanes(y, half)], w1o, wsem.at[5]),
         pltpu.make_async_copy(w2_ref, w2, wsem.at[6]),
     ]
-    for load in loads[:6]:
+    for load in loads[:5]:
         load.start()
 
     barrier = pltpu.get_barrier_semaphore()
@@ -129,8 +129,8 @@
         if j < 2:
             x_part(j, ax)
 
+    loads[5].start()
     loads[4].wait()
-    loads[6].start()
 
     def chunk(u):
         place = (u - 2) // 2
@@ -181,6 +181,7 @@
             @pl.when(start)
             def _():
                 loads[5].wait()
+                loads[6].start()
 
         co[pl.ds(n, count)] = product(xv, w1o, count)
 
@@ -383,8 +384,6 @@
     for kind, u in TAIL:
         tail(kind, u)
 
-    arrived(o_ref, orr)
-    sent(ob.at[pl.ds(0, 6)], oss)
     sent(cs, css)
     for sem, width in ((hys, half), (hxs, 2 * half), (hcs, 4 * half)):
         sent(hb.at[:, :, pl.ds(0, width)], sem)
@@ -401,6 +400,9 @@
     def _():
         sent(xb.at[pl.ds(0, 8), :, 0], xfs)
         sent(xb.at[pl.ds(0, 12), :, 0], xbs)
+
+    sent(ob.at[pl.ds(0, 6)], oss)
+    arrived(o_ref, orr)
 
 
 def solution(mesh):

time: 104 us -> 104 us (level)
  no operation moved by 1% of the time
where the time goes in v8:
time: 104 us
  Pallas kernels  104 us (100%)
    pallas_call x1, Pallas kernels, body(): pl.pallas_call(kernel, out_shape=jax.ShapeDtypeStruct((4, r // 4, d), bf1...  104 us

profile of v8, /device:TPU:0, one launch (start us, length us, event | category | flops | bytes accessed | tf_op | source)
XLA Modules:
  0.0 104.3 jit_solution(357925558384716782)
XLA Ops:
  0.0 103.5 %mlp.1 = bf16[4,16,2560]{2,1,0:T(8,128)(2,1)S(1)} custom-call(bf16[64,2560]{1,0:T(8,128)(2,1)} %x_ref.1, bf16[2560,1280]{1,0:T(8,128)(2,1)} %w1_ref.1, bf16[5120,640]{1,0:T(8,128)(2,1)} %w2_ref.1), custom_call_target="tpu_custom_call" | custom-call | tf_op jit(solution)/shard_map/mlp/pallas_call | solution.py:417
  103.5 0.7 copy.5

commit v9 on v7

--- a/solution.py
+++ b/solution.py
@@ -150,7 +150,7 @@
         z = jnp.dot(xv.reshape(count * ROWS, xv.shape[-1]), w[...], preferred_element_type=jnp.float32)
         return z.reshape(count, ROWS, z.shape[1])
 
-    def layer1(n, count, start):
+    def layer1(n, count, start, split):
         g, h = n // 2, lax.rem(n, 2)
         if count == 2:
             arrived(xb.at[g, :, 1 - core], xc2r.at[g])
@@ -165,7 +165,7 @@
                 cs[n, rows] = jnp.dot(xb[g, h, c], w1s[...], preferred_element_type=jnp.float32)
                 rcopy(cs.at[n, rows], cr.at[n, rows], css, crr.at[n], ypeer).start()
 
-            part(core)
+            pl.when(split)(lambda: part(core))
 
             @pl.when(h == ax)
             def _():
@@ -175,7 +175,13 @@
             def _():
                 arrived(xb.at[g, h, 1 - core], xc1r.at[j])
 
-            part(1 - core)
+            pl.when(split)(lambda: part(1 - core))
+
+            @pl.when(jnp.logical_not(split))
+            def _():
+                cs[pl.ds(n, 1)] = product(xb[g, h], w1s, 1)
+                rcopy(rows_of(cs, n, 1), rows_of(cr, n, 1), css, crr.at[n], ypeer).start()
+
             xv = xb[g, h]
 
             @pl.when(start)
@@ -295,7 +301,7 @@
             def _():
                 event(u, 2)
 
-        each(s, lambda u, count: layer1(chunk1(u), count, s == 0))
+        each(s, lambda u, count: layer1(chunk1(u), count, s == 0, lax.rem(s, 2) == 0))
         each(s - LF, lambda u, count: pass_y(chunk1(u), count))
 
         @pl.when((s >= 1) & (s < 5))
@@ -383,8 +389,6 @@
     for kind, u in TAIL:
         tail(kind, u)
 
-    arrived(o_ref, orr)
-    sent(ob.at[pl.ds(0, 6)], oss)
     sent(cs, css)
     for sem, width in ((hys, half), (hxs, 2 * half), (hcs, 4 * half)):
         sent(hb.at[:, :, pl.ds(0, width)], sem)
@@ -401,6 +405,9 @@
     def _():
         sent(xb.at[pl.ds(0, 8), :, 0], xfs)
         sent(xb.at[pl.ds(0, 12), :, 0], xbs)
+
+    sent(ob.at[pl.ds(0, 6)], oss)
+    arrived(o_ref, orr)
 
 
 def solution(mesh):

time: 104 us -> 104 us (level)
  no operation moved by 1% of the time
where the time goes in v9:
time: 104 us
  Pallas kernels  103 us (99%)
    pallas_call x1, Pallas kernels, body(): pl.pallas_call(kernel, out_shape=jax.ShapeDtypeStruct((4, r // 4, d), bf1...  103 us

profile of v9, /device:TPU:0, one launch (start us, length us, event | category | flops | bytes accessed | tf_op | source)
XLA Modules:
  0.0 104.2 jit_solution(10459178077736186332)
XLA Ops:
  0.0 103.4 %mlp.1 = bf16[4,16,2560]{2,1,0:T(8,128)(2,1)S(1)} custom-call(bf16[64,2560]{1,0:T(8,128)(2,1)} %x_ref.1, bf16[2560,1280]{1,0:T(8,128)(2,1)} %w1_ref.1, bf16[5120,640]{1,0:T(8,128)(2,1)} %w2_ref.1), custom_call_target="tpu_custom_call" | custom-call | tf_op jit(solution)/shard_map/mlp/pallas_call | solution.py:422
  103.4 0.7 copy.5
